TPU v7x, 32 devices: a whole 2x2x4 slice. The times are simulated.
32 devices in a mesh: rows: 8 (over z, y), feat: 4 (over x, core).
Axes of the slice: x: 2, y: 2, z: 4, core: 2. Of those that a mesh axis runs over, the one named last changes fastest.
Arguments:
- features: float32 [100, 8192], P('feat', 'rows'), may hold values from -12 to 12
- tiles: float32 [1024, 128, 128], P('rows'), may hold values from 0 to 1.5
- tile_slot: int32 [1024], P('rows'), may hold values from 0 to 15, as said below
- send_blocks: int32 [8, 8, 1], P('rows'), may hold values from 0 to 7
Outputs:
- ranked: float32 [100, 8192], P('feat', 'rows')
- change: float32 [4], replicated
Inputs may be any that keep to these rules, and one draw needn't show every extreme that they name: `tile_slot`: among the tiles of one index of rows, every received slot (8 to 15) is named by at least one tile.
All inputs are finite; a program needn't handle non-finite values.
Results may differ from a plain program's by a relative error of at most 0.0001.
Values sent between devices are 32-bit elements; how exact they have to be, the bound alone decides.
A program may use at most 128 MiB of HBM per device.

v0:
```python
import jax
import jax.numpy as jnp
from jax import lax
from jax.sharding import PartitionSpec as P

ITERS = 4


teleport = 0.15


def shards(features, tiles, tile_slot, send_blocks):
    width_dev, node_count = features.shape
    tile_size = tiles.shape[1]
    block_count = node_count // tile_size
    per_block = tiles.shape[0] // block_count
    peer_count = lax.axis_size("rows")
    slot_count = send_blocks.shape[2]
    total_nodes = node_count * peer_count
    total_width = width_dev * lax.axis_size("feat")
    degree = 1.0 + jnp.sum(tiles, axis=2).reshape(block_count, per_block, tile_size).sum(axis=1)
    start = features.reshape(width_dev, block_count, tile_size).transpose(1, 0, 2)
    outgoing_ids = send_blocks[0].reshape(-1)
    current = start
    partials = []
    for iteration in range(ITERS):
        outgoing = current[outgoing_ids].reshape(peer_count, slot_count, width_dev, tile_size)
        received = lax.all_to_all(outgoing, "rows", split_axis=0, concat_axis=0, tiled=True)
        halo = received.reshape(peer_count * slot_count, width_dev, tile_size)
        buffer = jnp.concatenate([current, halo], axis=0)
        picked = buffer[tile_slot]
        product = jnp.einsum("tij,tfj->tfi", tiles, picked, precision=lax.Precision.HIGHEST)
        summed = product.reshape(block_count, per_block, width_dev, tile_size).sum(axis=1)
        updated = (1.0 - teleport) * (current + summed) / degree[:, None, :] + teleport * start
        partial_value = jnp.sum((updated - current) ** 2) / (total_width * total_nodes)
        partials.append(lax.psum(partial_value, ("rows", "feat")))
        current = updated
    change = jnp.stack(partials)
    ranked = current.transpose(1, 0, 2).reshape(width_dev, node_count)
    return (ranked, change)


def solution(mesh):
    return jax.shard_map(
        shards,
        mesh=mesh,
        in_specs=(P("feat", "rows"), P("rows", None, None), P("rows"), P("rows", None, None)),
        out_specs=(P("feat", "rows"), P()),
        check_vma=False,
    )
```

profile of v0, /device:TPU:0, one launch (start us, length us, event | category | flops | bytes accessed | tf_op | source)
XLA Modules:
  0.0 164.5 jit_solution(2037960440983145954)
XLA Ops:
  0.6 0.7 fusion.12
  1.3 0.9 copy.87
  2.3 0.6 gather_fusion
  2.8 0.7 copy.67
  3.6 7.3 %all-to-all-start = ((f32[8,1,25,128]{3,1,2,0:T(1,128)}), f32[8,1,25,128]{3,1,2,0:T(1,128)S(1)}, u32[]{:S(2)}, u32[]{:S(2)}) async-start(f32[8,1,25,128]{3,1,2,0:T(1,128)} %copy.67), calls=%async_computation | async-start | bytes 204800 | tf_op jit(solution)/shard_map/all_to_all | solution.py:28
  10.9 0.7 compare_select_fusion
  11.6 5.6 %reduce_sum.100 = f32[128,128]{1,0:T(8,128)S(1)} reduce(f32[128,128,128]{2,1,0:T(8,128)} %param.5, f32[]{:T(128)} %constant.6.clone.1), dimensions={2}, to_apply=%region_1.0 | reduce | flops 2080768 | bytes 8454148 | tf_op jit(solution)/shard_map/reduce_sum | solution.py:21
  17.2 0.8 all-to-all-done
  18.1 0.8 gather_fusion.1
  18.9 15.4 %bitcast_reduce_fusion.3 = f32[8,25,128]{2,1,0:T(8,128)S(1)} fusion(f32[128,25,128]{2,1,0:T(8,128)S(1)} %gather_fusion.1, f32[128,128,128]{2,1,0:T(8,128)} %param.5), kind=kOutput, calls=%fused_computation.11 | convolution fusion | flops 629529600 | bytes 10129408 | tf_op jit(solution)/shard_map/tij,tfj->tfi/dot_general | solution.py:32
  35.0 12.1 %all_to_all.20 = f32[8,1,25,128]{3,1,2,0:T(1,128)S(1)} all-to-all(f32[8,1,25,128]{3,1,2,0:T(1,128)S(1)} %copy.71), channel_id=1, replica_groups=mesh['rows'=8,'feat'=4] {'rows'}, dimensions={0} | all-to-all | bytes 204800 | tf_op jit(solution)/shard_map/all_to_all | solution.py:28
  47.2 0.8 gather_fusion.3
  48.0 15.4 %bitcast_reduce_fusion.2 = f32[8,25,128]{2,1,0:T(8,128)S(1)} fusion(f32[128,25,128]{2,1,0:T(8,128)S(1)} %gather_fusion.3, f32[128,128,128]{2,1,0:T(8,128)} %param.5), kind=kOutput, calls=%fused_computation.10 | convolution fusion | flops 629529600 | bytes 10129408 | tf_op jit(solution)/shard_map/tij,tfj->tfi/dot_general | solution.py:32
  63.4 0.6 gather_fusion.4
  64.1 9.5 %all_to_all.21 = f32[8,1,25,128]{3,1,2,0:T(1,128)S(1)} all-to-all(f32[8,1,25,128]{3,1,2,0:T(1,128)S(1)} %copy.75), channel_id=1, replica_groups=mesh['rows'=8,'feat'=4] {'rows'}, dimensions={0} | all-to-all | bytes 204800 | tf_op jit(solution)/shard_map/all_to_all | solution.py:28
  73.7 0.8 gather_fusion.5
  74.5 15.4 %bitcast_reduce_fusion.1 = f32[8,25,128]{2,1,0:T(8,128)S(1)} fusion(f32[128,25,128]{2,1,0:T(8,128)S(1)} %gather_fusion.5, f32[128,128,128]{2,1,0:T(8,128)} %param.5), kind=kOutput, calls=%fused_computation.9 | convolution fusion | flops 629529600 | bytes 10129408 | tf_op jit(solution)/shard_map/tij,tfj->tfi/dot_general | solution.py:32
  90.6 9.5 %all_to_all.22 = f32[8,1,25,128]{3,1,2,0:T(1,128)S(1)} all-to-all(f32[8,1,25,128]{3,1,2,0:T(1,128)S(1)} %copy.79), channel_id=1, replica_groups=mesh['rows'=8,'feat'=4] {'rows'}, dimensions={0} | all-to-all | bytes 204800 | tf_op jit(solution)/shard_map/all_to_all | solution.py:28
  100.2 0.8 gather_fusion.7
  101.0 15.4 %bitcast_reduce_fusion = f32[8,25,128]{2,1,0:T(8,128)S(1)} fusion(f32[128,25,128]{2,1,0:T(8,128)S(1)} %gather_fusion.7, f32[128,128,128]{2,1,0:T(8,128)} %param.5), kind=kOutput, calls=%fused_computation.8 | convolution fusion | flops 629529600 | bytes 10129408 | tf_op jit(solution)/shard_map/tij,tfj->tfi/dot_general | solution.py:32
  116.4 0.7 multiply_reduce_fusion.3
  119.9 0.7 copy.88
  120.6 40.9 %all-reduce = (f32[1]{0:T(128)}, f32[1]{0:T(128)}, f32[1]{0:T(128)}, f32[1]{0:T(128)}) all-reduce(f32[1]{0:T(128)} %bitcast.27, f32[1]{0:T(128)} %bitcast.26, f32[1]{0:T(128)} %bitcast.25, f32[1]{0:T(128)} %bitcast.24), channel_id=1, replica_groups=mesh['rows'=8,'feat'=4] {'rows','feat'}, use_global_device_ids=true, to_apply=%region_13.0 | all-reduce | flops 4 | bytes 32 | tf_op jit(solution)/shard_map/psum | solution.py:36
  161.5 3.0 %pad_maximum_fusion.4 = f32[4]{0:T(128)} fusion(f32[1]{0:T(128)} %get-tuple-element.6, f32[1]{0:T(128)} %get-tuple-element.7, f32[1]{0:T(128)} %get-tuple-element.8, f32[1]{0:T(128)} %get-tuple-element.9), kind=kLoop, calls=%fused_computation.51 | loop fusion | flops 12 | bytes 32 | tf_op jit(solution)/shard_map/stack | solution.py:38
  (24 shorter events, 2.1 us)
Async XLA Ops:
  3.6 14.5 %all-to-all-start = ((f32[8,1,25,128]{3,1,2,0:T(1,128)}), f32[8,1,25,128]{3,1,2,0:T(1,128)S(1)}, u32[]{:S(2)}, u32[]{:S(2)}) async-start(f32[8,1,25,128]{3,1,2,0:T(1,128)} %copy.67), calls=%async_computation | async-start | bytes 204800 | tf_op jit(solution)/shard_map/all_to_all | solution.py:28
where the time goes:
time: 165 us; the launch traced here: 164 us
  blocking collectives  72.1 us (44%)
  matrix products  61.5 us (37%)
  other arithmetic  11.2 us (7%)
  local copies, waits for them, and re-layouts  8.15 us (5%)
  starting transfers between devices  7.31 us (4%)
  between operations  3.33 us (2%)
    dot_general x4, matrix products, shards(): jnp.einsum('tij,tfj->tfi', tiles, picked, precision=lax.Precision.HIGHEST)  61.5 us
    psum x1, blocking collectives, shards(): partials.append(lax.psum(partial_value, ('rows', 'feat')))  40.9 us
    all_to_all x3, blocking collectives, shards(): lax.all_to_all(outgoing, 'rows', split_axis=0, concat_axis=0, tiled=True)  31.2 us
    all_to_all x1, starting transfers between devices, shards(): lax.all_to_all(outgoing, 'rows', split_axis=0, concat_axis=0, tiled=True)  7.31 us
    reduce_sum x2, other arithmetic, shards(): jnp.sum(tiles, axis=2).reshape(block_count, per_block, tile_size)  5.63 us
  transfers between devices with their start and end apart: 1, of which 1 were waited for; matrix products, arithmetic and copies ran while one was open for 4% of the time, Pallas kernels for 0%

commit v1 on v0

v1 whole, which is shorter than its diff:
```python
import functools

import jax
import jax.numpy as jnp
from jax import lax
from jax.experimental import pallas as pl
from jax.experimental.pallas import tpu as pltpu
from jax.sharding import PartitionSpec as P

ITERS = 4
TELEPORT = 0.15
TRANSPOSED = True
MESH = pl.DeviceIdType.MESH


def split(value):
    high = value.astype(jnp.bfloat16)
    low = (value - high.astype(jnp.float32)).astype(jnp.bfloat16)
    return high, low


def kernel(
    peers, feats, total_count,
    features_ref, tiles_ref, slot_ref, send_ref,
    ranked_ref, change_ref,
    tile_buf, high_buf, low_buf, start, current, inverse, picks, outgoing, halo, change_out, change_in,
    tile_sem, send_sem, recv_sem, change_send_sem, change_recv_sem,
):
    width = features_ref.shape[0]
    blocks, padded, tile = current.shape
    per_block = tiles_ref.shape[0] // blocks
    slots = send_ref.shape[0]
    row = lax.axis_index("rows")
    col = lax.axis_index("feat")
    me = row * feats + col
    devices = peers * feats

    def tile_copy(block):
        part = pl.ds(block * per_block, per_block)
        return pltpu.make_async_copy(tiles_ref.at[part], tile_buf.at[part], tile_sem.at[block])

    for block in range(blocks):
        tile_copy(block).start()

    def greet(step, carry):
        other = lax.rem(me + step, devices)
        pl.semaphore_signal(
            barrier, inc=1, device_id={"rows": other // feats, "feat": lax.rem(other, feats)}, device_id_type=MESH
        )
        return carry

    barrier = pltpu.get_barrier_semaphore()
    lax.fori_loop(1, devices, greet, 0)

    def own_picks(block, value):
        high, low = split(value)
        picks[block, :padded] = high
        picks[block, padded:] = low

    ones_row = lax.broadcasted_iota(jnp.int32, (padded, tile), 0) == width
    for block in range(blocks):
        start[block] = jnp.where(ones_row, 1.0, 0.0)
        start[block, :width] = features_ref[:, block * tile : (block + 1) * tile]
        value = start[block]
        current[block] = value
        own_picks(block, value)

    def halo_copy(iteration, source, target, step):
        return pltpu.make_async_remote_copy(
            src_ref=outgoing.at[iteration, target],
            dst_ref=halo.at[iteration, source],
            send_sem=send_sem.at[iteration, target],
            recv_sem=recv_sem.at[iteration, source],
            device_id={"rows": target},
            device_id_type=MESH,
        )

    def fill(iteration):
        def body(peer, carry):
            for k in range(slots):
                outgoing[iteration, peer, k] = current[send_ref[k, peer]]
            return carry

        lax.fori_loop(0, peers, body, 0)
        for k in range(slots):
            halo[iteration, row, k] = outgoing[iteration, row, k]

    def send(iteration):
        def body(step, carry):
            halo_copy(iteration, row, lax.rem(row + step, peers), step).start()
            return carry

        lax.fori_loop(1, peers, body, 0)

    def receive(iteration):
        def body(step, carry):
            source = lax.rem(row + peers - step, peers)
            halo_copy(iteration, source, source, step).wait_recv()
            return carry

        lax.fori_loop(1, peers, body, 0)

        def unpack(peer, carry):
            for k in range(slots):
                own_picks(blocks + peer * slots + k, halo[iteration, peer, k])
            return carry

        lax.fori_loop(0, peers, unpack, 0)

    def drain(iteration):
        def body(step, carry):
            target = lax.rem(row + step, peers)
            halo_copy(iteration, row, target, step).wait_send()
            return carry

        lax.fori_loop(1, peers, body, 0)

    def product(block):
        gathered = [picks[slot_ref[block * per_block + t]] for t in range(per_block)]
        left = jnp.concatenate(gathered, axis=1)
        if TRANSPOSED:
            dims = (((1,), (0,)), ((), ()))
        else:
            dims = (((1,), (1,)), ((), ()))
        main = lax.dot_general(left, high_buf[block], dims, preferred_element_type=jnp.float32)
        rest = lax.dot_general(left[:padded], low_buf[block], dims, preferred_element_type=jnp.float32)
        return main[:padded] + main[padded:] + rest

    def iterate(iteration, first):
        squares = jnp.zeros((padded, tile), jnp.float32)
        fresh = []
        for block in range(blocks):
            summed = product(block)
            if first:
                scale = (1.0 - TELEPORT) / (1.0 + summed[width : width + 1])
                inverse[block] = jnp.broadcast_to(scale, inverse.shape[1:])
            else:
                scale = inverse[block, :1]
            before = current[block]
            after = (before + summed) * scale + TELEPORT * start[block]
            difference = after - before
            squares = squares + difference * difference
            fresh.append(after)
        for block in range(blocks):
            current[block] = fresh[block]
        feature_row = lax.broadcasted_iota(jnp.int32, (padded, tile), 0) < width
        squares = jnp.sum(jnp.where(feature_row, squares, 0.0))
        lane = lax.broadcasted_iota(jnp.int32, (1, tile), 1)
        return jnp.where(lane == iteration, squares, 0.0)

    fill(0)
    pl.semaphore_wait(barrier, devices - 1)
    send(0)

    for block in range(blocks):
        tile_copy(block).wait()
        for t in range(per_block):
            value = tile_buf[block * per_block + t]
            part = pl.ds(t * tile, tile)
            if TRANSPOSED:
                high, low = split(value.T)
                high_buf[block, part, :] = high
                low_buf[block, part, :] = low
            else:
                high, low = split(value)
                high_buf[block, :, part] = high
                low_buf[block, :, part] = low

    receive(0)
    changes = iterate(0, True)

    def later(iteration, changes):
        fill(iteration)
        send(iteration)
        for block in range(blocks):
            own_picks(block, current[block])
        receive(iteration)
        return changes + iterate(iteration, False)

    changes = lax.fori_loop(1, ITERS, later, changes)
    change_out[0] = changes
    for block in range(blocks):
        ranked_ref[:, block * tile : (block + 1) * tile] = current[block, :width]

    def change_copy(source, target):
        return pltpu.make_async_remote_copy(
            src_ref=change_out.at[0],
            dst_ref=change_in.at[source],
            send_sem=change_send_sem.at[target],
            recv_sem=change_recv_sem.at[source],
            device_id={"rows": target // feats, "feat": lax.rem(target, feats)},
            device_id_type=MESH,
        )

    def share(step, carry):
        change_copy(me, lax.rem(me + step, devices)).start()
        return carry

    lax.fori_loop(1, devices, share, 0)
    change_in[me] = changes
    for iteration in range(ITERS):
        drain(iteration)

    def collect(step, carry):
        source = lax.rem(me + devices - step, devices)
        change_copy(source, source).wait_recv()
        return carry

    lax.fori_loop(1, devices, collect, 0)
    change_ref[...] = jnp.sum(change_in[...], axis=0) * (1.0 / total_count)

    def finish(step, carry):
        target = lax.rem(me + step, devices)
        change_copy(me, target).wait_send()
        return carry

    lax.fori_loop(1, devices, finish, 0)


def solution(mesh):
    peers, feats = mesh.shape["rows"], mesh.shape["feat"]

    def shards(features, tiles, tile_slot, send_blocks):
        width, nodes = features.shape
        tile = tiles.shape[1]
        blocks = nodes // tile
        per_block = tiles.shape[0] // blocks
        slots = send_blocks.shape[2]
        padded = (width // 16 + 1) * 16
        total_count = width * feats * nodes * peers
        depth = per_block * tile
        devices = peers * feats
        split_shape = (blocks, depth, tile) if TRANSPOSED else (blocks, tile, depth)
        vmem = pl.BlockSpec(memory_space=pltpu.VMEM)
        smem = pl.BlockSpec(memory_space=pltpu.SMEM)
        ranked, change = pl.pallas_call(
            functools.partial(kernel, peers, feats, total_count),
            out_shape=(
                jax.ShapeDtypeStruct((width, nodes), jnp.float32),
                jax.ShapeDtypeStruct((1, tile), jnp.float32),
            ),
            in_specs=[vmem, pl.BlockSpec(memory_space=pl.ANY), smem, smem],
            out_specs=(vmem, vmem),
            scratch_shapes=[
                pltpu.VMEM(tiles.shape, jnp.float32),
                pltpu.VMEM(split_shape, jnp.bfloat16),
                pltpu.VMEM(split_shape, jnp.bfloat16),
                pltpu.VMEM((blocks, padded, tile), jnp.float32),
                pltpu.VMEM((blocks, padded, tile), jnp.float32),
                pltpu.VMEM((blocks, 8, tile), jnp.float32),
                pltpu.VMEM((blocks + peers * slots, 2 * padded, tile), jnp.bfloat16),
                pltpu.VMEM((ITERS, peers, slots, padded, tile), jnp.float32),
                pltpu.VMEM((ITERS, peers, slots, padded, tile), jnp.float32),
                pltpu.VMEM((1, 1, tile), jnp.float32),
                pltpu.VMEM((devices, 1, tile), jnp.float32),
                pltpu.SemaphoreType.DMA((blocks,)),
                pltpu.SemaphoreType.DMA((ITERS, peers)),
                pltpu.SemaphoreType.DMA((ITERS, peers)),
                pltpu.SemaphoreType.DMA((devices,)),
                pltpu.SemaphoreType.DMA((devices,)),
            ],
            compiler_params=pltpu.CompilerParams(collective_id=0, has_side_effects=True),
        )(features, tiles, tile_slot, send_blocks[0].T)
        return ranked, change[0, :ITERS]

    return jax.shard_map(
        shards,
        mesh=mesh,
        in_specs=(P("feat", "rows"), P("rows", None, None), P("rows"), P("rows", None, None)),
        out_specs=(P("feat", "rows"), P()),
        check_vma=False,
    )
```

time: 165 us -> 43.4 us (0.26)
  blocking collectives: 72.1 us -> 0 us
  matrix products: 61.5 us -> 0 us
  Pallas kernels: 0 us -> 39.8 us
  other arithmetic: 11.2 us -> 0 us
  starting transfers between devices: 7.31 us -> 0 us
  local copies, waits for them, and re-layouts: 8.15 us -> 2.74 us
  between operations: 3.33 us -> 0.64 us
    dot_general x4 -> x0, matrix products: 61.5 us -> none  [shards(): jnp.einsum('tij,tfj->tfi', tiles, picked, precision=lax.Precision.HIGHEST)]
    psum x1 -> x0, blocking collectives: 40.9 us -> none  [shards(): partials.append(lax.psum(partial_value, ('rows', 'feat')))]
    pallas_call x0 -> x1, Pallas kernels: none -> 39.8 us  [shards(): pl.pallas_call(functools.partial(kernel, peers, feats, total_count), out_...]
    all_to_all x3 -> x0, blocking collectives: 31.2 us -> none  [shards(): lax.all_to_all(outgoing, 'rows', split_axis=0, concat_axis=0, tiled=True)]
    all_to_all x1 -> x0, starting transfers between devices: 7.31 us -> none  [shards(): lax.all_to_all(outgoing, 'rows', split_axis=0, concat_axis=0, tiled=True)]
    reduce_sum x3 -> x0, other arithmetic: 6.36 us -> none  [the longest x2 5.63 us: shards(): jnp.sum(tiles, axis=2).reshape(block_count, per_block, tile_size)]
    gather x8 -> x0, local copies, waits for them, and re-layouts: 5.39 us -> none  [the longest x4 3.16 us: shards(): picked = buffer[tile_slot]]
    another operation x1 -> x0, other arithmetic: 3 us -> none  [shards(): change = jnp.stack(partials)]
  transfers between devices with their start and end apart: 1 -> 0, of which waited for: 1 -> 0; matrix products, arithmetic and copies ran while one was open for 4% -> 0% of each run, Pallas kernels for 0% -> 0%
where the time goes in v1:
time: 43.4 us; the launch traced here: 43.2 us
  Pallas kernels  39.8 us (92%)
  local copies, waits for them, and re-layouts  2.74 us (6%)
  between operations  0.64 us (1%)
    pallas_call x1, Pallas kernels, shards(): pl.pallas_call(functools.partial(kernel, peers, feats, total_count), out_...  39.8 us
    unnamed x1, local copies, waits for them, and re-layouts  1.57 us
    squeeze x1, local copies, waits for them, and re-layouts, shards(): return (ranked, change[0, :ITERS])  1.18 us

profile of v1, /device:TPU:0, one launch (start us, length us, event | category | flops | bytes accessed | tf_op | source)
XLA Modules:
  0.0 43.2 jit_solution(12727563574645908284)
XLA Ops:
  0.6 39.8 %shard_map.59 = (f32[25,1024]{1,0:T(8,128)}, f32[1,128]{1,0:T(1,128)}) custom-call(f32[25,1024]{1,0:T(8,128)} %features_ref.1, f32[128,128,128]{2,1,0:T(8,128)} %tiles_ref.1, s32[128]{0:T(128)} %slot_ref.1, s32[1,8]{1,0:T(1,128)} %bitcast.3), custom_call_target="tpu_custom_call" | custom-call | tf_op jit(solution)/shard_map/pallas_call | solution.py:236
  40.5 1.2 %slice_bitcast_fusion = f32[4]{0:T(128)} fusion(f32[1,128]{1,0:T(1,128)} %get-tuple-element.5), kind=kLoop, calls=%fused_computation | loop fusion | bytes 32 | tf_op jit(solution)/shard_map/squeeze | solution.py:264
  41.7 1.6 %copy.7 = f32[25,1024]{1,0:T(8,128)} copy(f32[25,1024]{1,0:T(8,128)} %get-tuple-element.8) | data formatting | bytes 204800

commit v2 on v1

--- a/solution.py
+++ b/solution.py
@@ -21,9 +21,9 @@
 
 def kernel(
     peers, feats, total_count,
-    features_ref, tiles_ref, slot_ref, send_ref,
+    features_hbm, tiles_ref, slot_hbm, send_hbm,
     ranked_ref, change_ref,
-    tile_buf, high_buf, low_buf, start, current, inverse, picks, outgoing, halo, change_out, change_in,
+    features_ref, slot_ref, send_ref, input_sem, tile_buf, high_buf, low_buf, start, current, inverse, picks, outgoing, halo, change_out, change_in,
     tile_sem, send_sem, recv_sem, change_send_sem, change_recv_sem,
 ):
     width = features_ref.shape[0]
@@ -34,29 +34,43 @@
     col = lax.axis_index("feat")
     me = row * feats + col
     devices = peers * feats
+    half = peers // 2
+    upper = row // half
+    near_count = peers - half
 
     def tile_copy(block):
         part = pl.ds(block * per_block, per_block)
         return pltpu.make_async_copy(tiles_ref.at[part], tile_buf.at[part], tile_sem.at[block])
 
+    inputs = [
+        pltpu.make_async_copy(features_hbm, features_ref, input_sem.at[0]),
+        pltpu.make_async_copy(send_hbm, send_ref, input_sem.at[1]),
+        pltpu.make_async_copy(slot_hbm, slot_ref, input_sem.at[2]),
+    ]
+    for copy in inputs:
+        copy.start()
+
+    def greet(step, carry):
+        other = lax.rem(row + step, peers)
+        pl.semaphore_signal(barrier, inc=1, device_id={"rows": other}, device_id_type=MESH)
+        return carry
+
+    barrier = pltpu.get_barrier_semaphore()
+    lax.fori_loop(1, peers, greet, 0)
+    for step in range(1, feats):
+        other = lax.rem(col + step, feats)
+        pl.semaphore_signal(barrier, inc=1, device_id={"feat": other}, device_id_type=MESH)
     for block in range(blocks):
         tile_copy(block).start()
-
-    def greet(step, carry):
-        other = lax.rem(me + step, devices)
-        pl.semaphore_signal(
-            barrier, inc=1, device_id={"rows": other // feats, "feat": lax.rem(other, feats)}, device_id_type=MESH
-        )
-        return carry
-
-    barrier = pltpu.get_barrier_semaphore()
-    lax.fori_loop(1, devices, greet, 0)
+    for copy in inputs:
+        copy.wait()
 
     def own_picks(block, value):
         high, low = split(value)
         picks[block, :padded] = high
         picks[block, padded:] = low
 
+    tail = jnp.where(lax.broadcasted_iota(jnp.int32, (padded - width, tile), 0) == 0, 1.0, 0.0)
     ones_row = lax.broadcasted_iota(jnp.int32, (padded, tile), 0) == width
     for block in range(blocks):
         start[block] = jnp.where(ones_row, 1.0, 0.0)
@@ -65,7 +79,7 @@
         current[block] = value
         own_picks(block, value)
 
-    def halo_copy(iteration, source, target, step):
+    def halo_copy(iteration, source, target):
         return pltpu.make_async_remote_copy(
             src_ref=outgoing.at[iteration, target],
             dst_ref=halo.at[iteration, source],
@@ -78,7 +92,7 @@
     def fill(iteration):
         def body(peer, carry):
             for k in range(slots):
-                outgoing[iteration, peer, k] = current[send_ref[k, peer]]
+                outgoing[iteration, peer, k] = current[send_ref[k, peer], :width]
             return carry
 
         lax.fori_loop(0, peers, body, 0)
@@ -86,31 +100,36 @@
             halo[iteration, row, k] = outgoing[iteration, row, k]
 
     def send(iteration):
-        def body(step, carry):
-            halo_copy(iteration, row, lax.rem(row + step, peers), step).start()
-            return carry
-
-        lax.fori_loop(1, peers, body, 0)
+        def across(step, carry):
+            far = step + (1 - upper) * (peers - 1 - 2 * step)
+            halo_copy(iteration, row, far).start()
+            return carry
+
+        def beside(step, carry):
+            near = upper * half + lax.rem(row - upper * half + step, near_count)
+            halo_copy(iteration, row, near).start()
+            return carry
+
+        lax.fori_loop(0, half, across, 0)
+        lax.fori_loop(1, near_count, beside, 0)
 
     def receive(iteration):
         def body(step, carry):
             source = lax.rem(row + peers - step, peers)
-            halo_copy(iteration, source, source, step).wait_recv()
+            halo_copy(iteration, source, source).wait_recv()
             return carry
 
         lax.fori_loop(1, peers, body, 0)
-
-        def unpack(peer, carry):
+        for peer in range(peers):
             for k in range(slots):
-                own_picks(blocks + peer * slots + k, halo[iteration, peer, k])
-            return carry
-
-        lax.fori_loop(0, peers, unpack, 0)
+                high, low = split(jnp.concatenate([halo[iteration, peer, k], tail], axis=0))
+                picks[blocks + peer * slots + k, :padded] = high
+                picks[blocks + peer * slots + k, padded:] = low
 
     def drain(iteration):
         def body(step, carry):
             target = lax.rem(row + step, peers)
-            halo_copy(iteration, row, target, step).wait_send()
+            halo_copy(iteration, row, target).wait_send()
             return carry
 
         lax.fori_loop(1, peers, body, 0)
@@ -149,7 +168,7 @@
         return jnp.where(lane == iteration, squares, 0.0)
 
     fill(0)
-    pl.semaphore_wait(barrier, devices - 1)
+    pl.semaphore_wait(barrier, peers + feats - 2)
     send(0)
 
     for block in range(blocks):
@@ -215,6 +234,12 @@
         return carry
 
     lax.fori_loop(1, devices, finish, 0)
+
+
+def finish_kernel(ranked_in, change_in, ranked_ref, change_ref):
+    ranked_ref[...] = ranked_in[...]
+    for iteration in range(ITERS):
+        change_ref[iteration] = change_in[0, iteration]
 
 
 def solution(mesh):
@@ -239,9 +264,13 @@
                 jax.ShapeDtypeStruct((width, nodes), jnp.float32),
                 jax.ShapeDtypeStruct((1, tile), jnp.float32),
             ),
-            in_specs=[vmem, pl.BlockSpec(memory_space=pl.ANY), smem, smem],
+            in_specs=[pl.BlockSpec(memory_space=pl.ANY)] * 4,
             out_specs=(vmem, vmem),
             scratch_shapes=[
+                pltpu.VMEM(features.shape, jnp.float32),
+                pltpu.SMEM(tile_slot.shape, jnp.int32),
+                pltpu.SMEM((slots, peers), jnp.int32),
+                pltpu.SemaphoreType.DMA((3,)),
                 pltpu.VMEM(tiles.shape, jnp.float32),
                 pltpu.VMEM(split_shape, jnp.bfloat16),
                 pltpu.VMEM(split_shape, jnp.bfloat16),
@@ -249,8 +278,8 @@
                 pltpu.VMEM((blocks, padded, tile), jnp.float32),
                 pltpu.VMEM((blocks, 8, tile), jnp.float32),
                 pltpu.VMEM((blocks + peers * slots, 2 * padded, tile), jnp.bfloat16),
-                pltpu.VMEM((ITERS, peers, slots, padded, tile), jnp.float32),
-                pltpu.VMEM((ITERS, peers, slots, padded, tile), jnp.float32),
+                pltpu.VMEM((ITERS, peers, slots, width, tile), jnp.float32),
+                pltpu.VMEM((ITERS, peers, slots, width, tile), jnp.float32),
                 pltpu.VMEM((1, 1, tile), jnp.float32),
                 pltpu.VMEM((devices, 1, tile), jnp.float32),
                 pltpu.SemaphoreType.DMA((blocks,)),
@@ -261,7 +290,15 @@
             ],
             compiler_params=pltpu.CompilerParams(collective_id=0, has_side_effects=True),
         )(features, tiles, tile_slot, send_blocks[0].T)
-        return ranked, change[0, :ITERS]
+        return pl.pallas_call(
+            finish_kernel,
+            out_shape=(
+                jax.ShapeDtypeStruct((width, nodes), jnp.float32),
+                jax.ShapeDtypeStruct((ITERS,), jnp.float32),
+            ),
+            in_specs=[vmem, smem],
+            out_specs=(vmem, smem),
+        )(ranked, change)
 
     return jax.shard_map(
         shards,

time: 43.4 us -> 38.8 us (0.89)
  local copies, waits for them, and re-layouts: 2.74 us -> 0 us
  Pallas kernels: 39.8 us -> 38 us
    pallas_call x1, Pallas kernels: 39.8 us -> 36.4 us  [shards(): pl.pallas_call(functools.partial(kernel, peers, feats, total_count), out_...]
    pallas_call x0 -> x1, Pallas kernels: none -> 1.59 us  [shards(): pl.pallas_call(finish_kernel, out_shape=(jax.ShapeDtypeStruct((width, nod...]
    unnamed x1 -> x0, local copies, waits for them, and re-layouts: 1.57 us -> none
    squeeze x1 -> x0, local copies, waits for them, and re-layouts: 1.18 us -> none  [shards(): return (ranked, change[0, :ITERS])]
where the time goes in v2:
time: 38.8 us; the launch traced here: 38.6 us
  Pallas kernels  38 us (98%)
  between operations  0.64 us (2%)
    pallas_call x1, Pallas kernels, shards(): pl.pallas_call(functools.partial(kernel, peers, feats, total_count), out_...  36.4 us
    pallas_call x1, Pallas kernels, shards(): pl.pallas_call(finish_kernel, out_shape=(jax.ShapeDtypeStruct((width, nod...  1.59 us

profile of v2, /device:TPU:0, one launch (start us, length us, event | category | flops | bytes accessed | tf_op | source)
XLA Modules:
  0.0 38.6 jit_solution(2073309843727913711)
XLA Ops:
  0.6 36.4 %shard_map.59 = (f32[25,1024]{1,0:T(8,128)}, f32[1,128]{1,0:T(1,128)}) custom-call(f32[25,1024]{1,0:T(8,128)} %features_hbm.1, f32[128,128,128]{2,1,0:T(8,128)} %tiles_ref.1, s32[128]{0:T(128)} %slot_hbm.1, s32[1,8]{1,0:T(1,128)} %bitcast.1), custom_call_target="tpu_custom_call" | custom-call | tf_op jit(solution)/shard_map/pallas_call | solution.py:261
  37.0 1.6 %shard_map.60 = (f32[25,1024]{1,0:T(8,128)}, f32[4]{0:T(128)}) custom-call(f32[25,1024]{1,0:T(8,128)} %get-tuple-element.4.ranked_in, f32[1,128]{1,0:T(1,128)} %get-tuple-element.5.change_in), custom_call_target="tpu_custom_call" | custom-call | tf_op jit(solution)/shard_map/pallas_call | solution.py:293

commit v3 on v2

--- a/solution.py
+++ b/solution.py
@@ -83,8 +83,8 @@
         return pltpu.make_async_remote_copy(
             src_ref=outgoing.at[iteration, target],
             dst_ref=halo.at[iteration, source],
-            send_sem=send_sem.at[iteration, target],
-            recv_sem=recv_sem.at[iteration, source],
+            send_sem=send_sem.at[iteration],
+            recv_sem=recv_sem.at[iteration],
             device_id={"rows": target},
             device_id_type=MESH,
         )
@@ -114,12 +114,8 @@
         lax.fori_loop(1, near_count, beside, 0)
 
     def receive(iteration):
-        def body(step, carry):
-            source = lax.rem(row + peers - step, peers)
-            halo_copy(iteration, source, source).wait_recv()
-            return carry
-
-        lax.fori_loop(1, peers, body, 0)
+        landed = halo.at[iteration, pl.ds(0, peers - 1)]
+        pltpu.make_async_copy(landed, landed, recv_sem.at[iteration]).wait()
         for peer in range(peers):
             for k in range(slots):
                 high, low = split(jnp.concatenate([halo[iteration, peer, k], tail], axis=0))
@@ -127,12 +123,8 @@
                 picks[blocks + peer * slots + k, padded:] = low
 
     def drain(iteration):
-        def body(step, carry):
-            target = lax.rem(row + step, peers)
-            halo_copy(iteration, row, target).wait_send()
-            return carry
-
-        lax.fori_loop(1, peers, body, 0)
+        left = outgoing.at[iteration, pl.ds(0, peers - 1)]
+        pltpu.make_async_copy(left, left, send_sem.at[iteration]).wait()
 
     def product(block):
         gathered = [picks[slot_ref[block * per_block + t]] for t in range(per_block)]
@@ -198,42 +190,42 @@
 
     changes = lax.fori_loop(1, ITERS, later, changes)
     change_out[0] = changes
-    for block in range(blocks):
-        ranked_ref[:, block * tile : (block + 1) * tile] = current[block, :width]
 
     def change_copy(source, target):
         return pltpu.make_async_remote_copy(
             src_ref=change_out.at[0],
             dst_ref=change_in.at[source],
-            send_sem=change_send_sem.at[target],
-            recv_sem=change_recv_sem.at[source],
+            send_sem=change_send_sem.at[0],
+            recv_sem=change_recv_sem.at[0],
             device_id={"rows": target // feats, "feat": lax.rem(target, feats)},
             device_id_type=MESH,
         )
 
-    def share(step, carry):
-        change_copy(me, lax.rem(me + step, devices)).start()
+    def share_across(step, carry):
+        change_copy(me, step + (1 - upper) * (devices - 1 - 2 * step)).start()
         return carry
 
-    lax.fori_loop(1, devices, share, 0)
+    def share_beside(step, carry):
+        base = upper * (devices // 2)
+        change_copy(me, base + lax.rem(me - base + step, devices - devices // 2)).start()
+        return carry
+
+    lax.fori_loop(0, devices // 2, share_across, 0)
+    lax.fori_loop(1, devices - devices // 2, share_beside, 0)
     change_in[me] = changes
+    for block in range(blocks):
+        features_ref[:, block * tile : (block + 1) * tile] = current[block, :width]
+    ranked_copy = pltpu.make_async_copy(features_ref, ranked_ref, input_sem.at[0])
+    ranked_copy.start()
     for iteration in range(ITERS):
         drain(iteration)
 
-    def collect(step, carry):
-        source = lax.rem(me + devices - step, devices)
-        change_copy(source, source).wait_recv()
-        return carry
-
-    lax.fori_loop(1, devices, collect, 0)
+    landed = change_in.at[pl.ds(0, devices - 1)]
+    pltpu.make_async_copy(landed, landed, change_recv_sem.at[0]).wait()
     change_ref[...] = jnp.sum(change_in[...], axis=0) * (1.0 / total_count)
 
-    def finish(step, carry):
-        target = lax.rem(me + step, devices)
-        change_copy(me, target).wait_send()
-        return carry
-
-    lax.fori_loop(1, devices, finish, 0)
+    pltpu.make_async_copy(landed, landed, change_send_sem.at[0]).wait()
+    ranked_copy.wait()
 
 
 def finish_kernel(ranked_in, change_in, ranked_ref, change_ref):
@@ -265,7 +257,7 @@
                 jax.ShapeDtypeStruct((1, tile), jnp.float32),
             ),
             in_specs=[pl.BlockSpec(memory_space=pl.ANY)] * 4,
-            out_specs=(vmem, vmem),
+            out_specs=(pl.BlockSpec(memory_space=pl.ANY), vmem),
             scratch_shapes=[
                 pltpu.VMEM(features.shape, jnp.float32),
                 pltpu.SMEM(tile_slot.shape, jnp.int32),
@@ -283,10 +275,10 @@
                 pltpu.VMEM((1, 1, tile), jnp.float32),
                 pltpu.VMEM((devices, 1, tile), jnp.float32),
                 pltpu.SemaphoreType.DMA((blocks,)),
-                pltpu.SemaphoreType.DMA((ITERS, peers)),
-                pltpu.SemaphoreType.DMA((ITERS, peers)),
-                pltpu.SemaphoreType.DMA((devices,)),
-                pltpu.SemaphoreType.DMA((devices,)),
+                pltpu.SemaphoreType.DMA((ITERS,)),
+                pltpu.SemaphoreType.DMA((ITERS,)),
+                pltpu.SemaphoreType.DMA((1,)),
+                pltpu.SemaphoreType.DMA((1,)),
             ],
             compiler_params=pltpu.CompilerParams(collective_id=0, has_side_effects=True),
         )(features, tiles, tile_slot, send_blocks[0].T)

time: 38.8 us -> 37 us (0.954)
  Pallas kernels: 38 us -> 36.3 us
    pallas_call x1, Pallas kernels: 36.4 us -> 34.7 us  [shards(): pl.pallas_call(functools.partial(kernel, peers, feats, total_count), out_...]
where the time goes in v3:
time: 37 us; the launch traced here: 36.9 us
  Pallas kernels  36.3 us (98%)
  between operations  0.64 us (2%)
    pallas_call x1, Pallas kernels, shards(): pl.pallas_call(functools.partial(kernel, peers, feats, total_count), out_...  34.7 us
    pallas_call x1, Pallas kernels, shards(): pl.pallas_call(finish_kernel, out_shape=(jax.ShapeDtypeStruct((width, nod...  1.59 us

profile of v3, /device:TPU:0, one launch (start us, length us, event | category | flops | bytes accessed | tf_op | source)
XLA Modules:
  0.0 36.9 jit_solution(1985713172526409020)
XLA Ops:
  0.6 34.7 %shard_map.59 = (f32[25,1024]{1,0:T(8,128)}, f32[1,128]{1,0:T(1,128)}) custom-call(f32[25,1024]{1,0:T(8,128)} %features_hbm.1, f32[128,128,128]{2,1,0:T(8,128)} %tiles_ref.1, s32[128]{0:T(128)} %slot_hbm.1, s32[1,8]{1,0:T(1,128)} %bitcast.1), custom_call_target="tpu_custom_call" | custom-call | tf_op jit(solution)/shard_map/pallas_call | solution.py:253
  35.3 1.6 %shard_map.60 = (f32[25,1024]{1,0:T(8,128)}, f32[4]{0:T(128)}) custom-call(f32[25,1024]{1,0:T(8,128)} %get-tuple-element.4.ranked_in, f32[1,128]{1,0:T(1,128)} %get-tuple-element.5.change_in), custom_call_target="tpu_custom_call" | custom-call | tf_op jit(solution)/shard_map/pallas_call | solution.py:285
